TPU v7x, 16 devices: a 4x2x1 block of a 4x4x4 slice. The times are simulated.
16 devices in a mesh: dp: 4 (over y, z, core), ep: 4 (over x).
Axes of the slice: x: 4, y: 2, z: 1, core: 2. Of those that a mesh axis runs over, the one named last changes fastest.
The devices are a block of a 4x4x4 slice.
Arguments:
- x: bfloat16 [4, 4, 384, 5120], P('dp', 'ep'), parts along dimension 0
- expert: int32 [4, 4, 384, 8], P('dp', 'ep'), parts along dimension 0
- slot: int32 [4, 4, 384, 8], P('dp', 'ep'), parts along dimension 0
- gate: float32 [4, 4, 384, 8], P('dp', 'ep'), parts along dimension 0
- w_gate: bfloat16 [40, 5120, 1536], P('ep')
- w_up: bfloat16 [40, 5120, 1536], P('ep')
- w_down: bfloat16 [40, 1536, 5120], P('ep')
- s_gate: bfloat16 [5120, 1536], replicated
- s_up: bfloat16 [5120, 1536], replicated
- s_down: bfloat16 [1536, 5120], replicated
Outputs:
- y: bfloat16 [4, 4, 384, 5120], P('dp', 'ep'), parts along dimension 0
There are 4 independent parts. A program takes and returns all parts, laid end to end along the dimension named above; an argument that names none is the same for every part.
All inputs are finite; a program needn't handle non-finite values.
Results may differ from a plain program's by a relative error of at most 0.009.
Values are sent between devices in bfloat16 or wider.
A program may use at most 1.5 GiB of HBM per device.

v0:
```python
import jax
import jax.numpy as jnp
from jax import lax
from jax.sharding import NamedSharding, PartitionSpec as P


def einsum(form, a, b):
    return jnp.einsum(form, a.astype(jnp.float32), b.astype(jnp.float32))


def for_all(x, s_gate, s_up, s_down):
    h = jax.nn.silu(einsum("...d,df->...f", x, s_gate)) * einsum("...d,df->...f", x, s_up)
    return einsum("...f,fd->...d", h.astype(jnp.bfloat16), s_down)


def solution(mesh):
    def placed(v, *spec):
        return lax.with_sharding_constraint(v, NamedSharding(mesh, P(*spec)))

    def step(x, expert, slot, gate, w_gate, w_up, w_down, s_gate, s_up, s_down):
        experts, (tokens, top) = w_gate.shape[0], expert.shape[2:]
        slots = 5 * tokens * top // (4 * experts)
        to_expert = jax.nn.one_hot(expert, experts, dtype=jnp.bfloat16)
        to_slot = jax.nn.one_hot(slot, slots, dtype=jnp.bfloat16)
        weighted = to_expert * gate[..., None].astype(jnp.bfloat16)
        dispatch = einsum("abtke,abtkc->abtec", to_expert, to_slot).astype(jnp.bfloat16)
        combine = einsum("abtke,abtkc->abtec", weighted, to_slot).astype(jnp.bfloat16)
        z = einsum("abtec,abtd->aebcd", dispatch, x).astype(jnp.bfloat16)
        z = placed(z, "dp", None, "ep", None, None)
        z = placed(z, "dp", "ep", None, None, None)
        h = jax.nn.silu(einsum("aebcd,edf->aebcf", z, w_gate))
        h = (h * einsum("aebcd,edf->aebcf", z, w_up)).astype(jnp.bfloat16)
        out = einsum("aebcf,efd->aebcd", h, w_down).astype(jnp.bfloat16)
        out = placed(out, "dp", "ep", None, None, None)
        out = placed(out, "dp", None, "ep", None, None)
        y = einsum("abtec,aebcd->abtd", combine, out)
        return (y + for_all(x, s_gate, s_up, s_down)).astype(jnp.bfloat16)

    return step
```

profile of v0, /device:TPU:112, one launch (start us, length us, event | category | flops | bytes accessed | tf_op | source)
XLA Modules:
  0.0 1210.1 jit_solution(9428081841612283092)
XLA Ops:
  0.0 0.8 copy.11
  0.8 0.0 copy-start
  0.8 0.9 copy.9
  1.7 0.0 copy-start.2
  1.7 4.3 convolution_convert_fusion.1
  6.0 27.4 %convolution_convert_fusion = bf16[40,96,5120]{2,1,0:T(8,128)(2,1)} fusion(bf16[1,1,384,5120]{3,2,1,0:T(8,128)(2,1)} %param.3, bf16[384,40,96]{2,1,0:T(8,128)(2,1)S(1)} %convolution_convert_fusion.1), kind=kOutput, calls=%fused_computation.11 | convolution fusion | flops 15119155200 | bytes 46202880 | tf_op jit(solution)/abtec,abtd->aebcd/dot_general | solution.py:8
  33.4 0.0 copy-done
  33.4 0.0 copy-done.2
  33.4 446.9 %all-to-all.4 = bf16[1,4,10,1,96,5120]{5,4,2,3,0,1:T(8,128)(2,1)} all-to-all(bf16[1,4,10,1,96,5120]{5,4,2,3,0,1:T(8,128)(2,1)} %bitcast.123), channel_id=1, replica_groups=mesh['dp'=4,'ep'=4] {'ep'}, dimensions={1} | all-to-all | bytes 78643200 | tf_op jit(solution)/sharding_constraint;jit(solution)/sharding_constraint | solution.py:18
  480.3 85.9 %bitcast_multiply_fusion.1 = f32[1,10,4,96,1536]{4,3,2,1,0:T(8,128)} fusion(bf16[10,5120,1536]{2,1,0:T(8,128)(2,1)} %param.4, bf16[1,4,10,1,96,5120]{5,4,2,3,0,1:T(8,128)(2,1)} %all-to-all.4), kind=kOutput, calls=%fused_computation.14 | convolution fusion | flops 60421570560 | bytes 220200960 | tf_op jit(solution)/aebcd,edf->aebcf/dot_general | solution.py:8
  566.2 78.6 %fusion.12 = bf16[1,10,4,96,1536]{4,3,2,1,0:T(8,128)(2,1)} fusion(f32[1,10,4,96,1536]{4,3,2,1,0:T(8,128)} %bitcast_multiply_fusion.1, bf16[10,5120,1536]{2,1,0:T(8,128)(2,1)} %param.5, bf16[1,4,10,1,96,5120]{5,4,2,3,0,1:T(8,128)(2,1)} %all-to-all.4), kind=kOutput, calls=%fused_computation.13 | convolution fusion | flops 60409774080 | bytes 231997440 | tf_op jit(solution)/aebcd,edf->aebcf/dot_general | solution.py:8
  644.8 79.3 %convert_bitcast_fusion = bf16[1,10,4,1,96,5120]{5,4,2,1,3,0:T(8,128)(2,1)} fusion(bf16[10,1536,5120]{2,1,0:T(8,128)(2,1)} %param.6, bf16[1,10,4,96,1536]{4,3,2,1,0:T(8,128)(2,1)} %fusion.12), kind=kOutput, calls=%fused_computation.8 | convolution fusion | flops 60417638400 | bytes 208404480 | tf_op jit(solution)/aebcf,efd->aebcd/dot_general | solution.py:8
  724.1 26.7 %copy.15 = bf16[1,10,4,1,96,5120]{5,4,1,3,0,2:T(8,128)(2,1)} copy(bf16[1,10,4,1,96,5120]{5,4,2,1,3,0:T(8,128)(2,1)} %convert_bitcast_fusion) | data formatting | bytes 78643200 | tf_op jit(solution)/sharding_constraint;jit(solution)/sharding_constraint | solution.py:18
  750.9 0.0 copy-start.3
  750.9 11.0 all-to-all-start.1
  761.9 0.0 copy-done.4
  761.9 0.2 copy.10
  762.0 0.0 copy-done.1
  762.1 0.0 copy-done.3
  762.1 6.0 convolution_convert_fusion.2
  768.0 10.6 fusion.40
  778.6 26.7 %fusion.50 = f32[384,5120]{1,0:T(8,128)} fusion(bf16[1536,5120]{1,0:T(8,128)(2,1)} %param.9, bf16[5120,1536]{1,0:T(8,128)(2,1)} %param.8, bf16[1,1,384,5120]{3,2,1,0:T(8,128)(2,1)} %param.3, f32[1,1,384,1536]{3,2,1,0:T(8,128)S(1)} %fusion.40), kind=kOutput, calls=%fused_computation.35 | convolution fusion | flops 12083134464 | bytes 45613056 | tf_op jit(solution)/...f,fd->...d/dot_general | solution.py:8
  805.3 381.3 %all-to-all-done.1 = bf16[1,10,4,1,96,5120]{5,4,1,3,0,2:T(8,128)(2,1)} async-done(((bf16[1,10,4,1,96,5120]{5,4,1,3,0,2:T(8,128)(2,1)}), bf16[1,10,4,1,96,5120]{5,4,1,3,0,2:T(8,128)(2,1)}, u32[]{:S(2)}, u32[]{:S(2)}) %all-to-all-start.1) | async-done | bytes 39321632 | tf_op jit(solution)/sharding_constraint;jit(solution)/sharding_constraint | solution.py:18
  1186.6 23.6 %fusion.26 = bf16[1,1,384,5120]{3,2,1,0:T(8,128)(2,1)} fusion(f32[384,5120]{1,0:T(8,128)} %fusion.50, bf16[40,96,5120]{2,1,0:T(8,128)(2,1)} %bitcast.25, bf16[384,40,96]{2,1,0:T(8,128)(2,1)} %convolution_convert_fusion.2), kind=kOutput, calls=%fused_computation.22 | convolution fusion | flops 15103426560 | bytes 54067200 | tf_op jit(solution)/abtec,aebcd->abtd/dot_general | solution.py:8
  (3 shorter events, 0.0 us)
Async XLA Ops:
  0.8 32.5 %copy-start = (s32[384,8]{1,0:T(8,128)}, s32[384,8]{1,0:T(8,128)S(1)}, u32[]{:S(2)}) copy-start(s32[384,8]{1,0:T(8,128)S(1)} %copy.11) | copy-start | bytes 36868
  1.7 31.7 %copy-start.2 = (s32[384,8]{1,0:T(8,128)}, s32[384,8]{1,0:T(8,128)S(1)}, u32[]{:S(2)}) copy-start(s32[384,8]{1,0:T(8,128)S(1)} %copy.9) | copy-start | bytes 36868
  750.9 11.0 copy-start.4
  750.9 11.2 copy-start.1
  750.9 11.2 copy-start.3
  750.9 435.7 %all-to-all-start.1 = ((bf16[1,10,4,1,96,5120]{5,4,1,3,0,2:T(8,128)(2,1)}), bf16[1,10,4,1,96,5120]{5,4,1,3,0,2:T(8,128)(2,1)}, u32[]{:S(2)}, u32[]{:S(2)}) async-start(bf16[1,10,4,1,96,5120]{5,4,1,3,0,2:T(8,128)(2,1)} %copy.15), calls=%async_computation.1 | async-start | bytes 78643200 | tf_op jit(solution)/sharding_constraint;jit(solution)/sharding_constraint | solution.py:18
where the time goes:
time: 1210 us
  blocking collectives  447 us (37%)
  waiting for transfers between devices  381 us (31%)
  matrix products  342 us (28%)
  local copies, waits for them, and re-layouts  28.6 us (2%)
    another operation x1, blocking collectives, placed(): return lax.with_sharding_constraint(v, NamedSharding(mesh, P(*spec)))  447 us
    another operation x1, waiting for transfers between devices, placed(): return lax.with_sharding_constraint(v, NamedSharding(mesh, P(*spec)))  381 us
    dot_general x9, matrix products, einsum(): return jnp.einsum(form, a.astype(jnp.float32), b.astype(jnp.float32))  342 us
    another operation x1, local copies, waits for them, and re-layouts, placed(): return lax.with_sharding_constraint(v, NamedSharding(mesh, P(*spec)))  26.7 us
  transfers between devices with their start and end apart: 1, of which 1 were waited for; matrix products, arithmetic and copies ran while one was open for 4% of the time, Pallas kernels for 0%

commit v1 on v0

v1 whole, which is shorter than its diff:
```python
import jax
import jax.numpy as jnp
from jax import lax
from jax.experimental import pallas as pl
from jax.experimental.pallas import tpu as pltpu
from jax.sharding import PartitionSpec as P

F32, BF16 = jnp.float32, jnp.bfloat16
MESH = pl.DeviceIdType.MESH
VMEM_BYTES = 67_000_000
X_COLUMNS, F_COLUMNS, X_RING = 512, 1536, 2
Y_COLUMNS, Y_RING, LAG = 512, 3, 3


def dot(a, b):
    return jnp.dot(a, b, preferred_element_type=F32)


def ring(members):
    me = lax.axis_index("ep")
    return me, lax.rem(me + 1, members), lax.rem(me + members - 1, members), lax.rem(me + 2, members)


def greet(*devices):
    barrier = pltpu.get_barrier_semaphore()
    for device in devices:
        pl.semaphore_signal(barrier, inc=1, device_id={"ep": device}, device_id_type=MESH)
    pl.semaphore_wait(barrier, len(devices))


def remote(src, dst, send, recv, device):
    return pltpu.make_async_remote_copy(
        src_ref=src, dst_ref=dst, send_sem=send, recv_sem=recv, device_id={"ep": device}, device_id_type=MESH
    )


def block(i, size):
    return pl.ds(pl.multiple_of(i * size, size), size)


def gather_kernel(
    members, x, meta, w_gate, w_up, s_gate, s_up, h, hs, xg, metas,
    acc_g, acc_u, xbuf, z, onehot, wbuf, hbuf, mbuf,
    s1s, s1r, s2s, s2r, ms, mr, wsem, xsem, hsem,
):
    (tokens, d), (local, rows, width) = x.shape, z.shape
    slots, half, chunks = rows // members, tokens // 2, d // width
    depth, fb = wbuf.shape[0], wbuf.shape[3]
    ff, hw, top = w_gate.shape[2], hbuf.shape[2], meta.shape[0] // 2
    nf = ff // fb
    head, steps = chunks * nf, local * nf
    me, right, left, across = ring(members)
    sides = (right, left)
    greet(right, left, across)

    def first(k, side):
        return remote(x.at[:, block(k, width)], xg.at[side, :, block(k, width)], s1s.at[k, side], s1r.at[k, side], sides[side])

    def second(k, side):
        part = pl.ds(side * half, half)
        return remote(
            xg.at[side, part, block(k, width)], xg.at[2, part, block(k, width)], s2s.at[k, side], s2r.at[k, side], sides[side]
        )

    def tell(i):
        return remote(meta, mbuf.at[i], ms.at[i], mr.at[i], (right, left, across)[i])

    def relay(k):
        for side in range(2):
            first(k, side).wait_recv()
        for side in range(2):
            second(k, side).start()

        @pl.when(k + 1 < chunks)
        def _():
            for side in range(2):
                first(k + 1, side).start()

    def weights(g, slot, start):
        def copies(gate, up):
            for i, src in enumerate((gate, up)):
                copy = pltpu.make_async_copy(src, wbuf.at[slot, i], wsem.at[slot, i])
                copy.start() if start else copy.wait()

        if not start:
            return copies(s_gate.at[:width, :fb], s_up.at[:width, :fb])

        @pl.when(g < head)
        def _():
            k, f = g // nf, g % nf
            copies(*(s.at[block(k, width), block(f, fb)] for s in (s_gate, s_up)))

        @pl.when((g >= head) & (g < head + chunks * steps))
        def _():
            k, i = (g - head) // steps, (g - head) % steps
            copies(*(w.at[i // nf, block(k, width), block(i % nf, fb)] for w in (w_gate, w_up)))

    def tokens_in(k, source, slot):
        src = x if source == 0 else xg.at[source - 1]
        return pltpu.make_async_copy(src.at[:, block(k, width)], xbuf.at[slot], xsem.at[slot])

    def put(dst, p):
        return pltpu.make_async_copy(hbuf.at[p], dst, hsem.at[p])

    def activate(zz, i, slot, dst, last, wait):
        for j in range(fb // hw):
            part = pl.ds(j * hw, hw)
            g, u = acc_g[i, :, part], acc_u[i, :, part]
            if last:
                g += dot(zz, wbuf[slot, 0, :, part])
                u += dot(zz, wbuf[slot, 1, :, part])
            v = (jax.nn.silu(g) * u).astype(BF16)
            p = (i % nf) * (fb // hw) + j
            if wait:
                put(hs.at[:, pl.ds(0, hw)], p).wait()
            hbuf[p] = v
            put(dst.at[:, block(p, hw)], p).start()

    for side in range(2):
        first(0, side).start()
    for i in range(members - 1):
        tell(i).start()
    for g in range(depth - 1):
        weights(jnp.int32(g), g, True)
    for k in range(members - 1):
        tokens_in(k, 0, k).start()

    @pl.loop(0, chunks)
    def _(k):
        slot_x = k % members

        @pl.when(k + members - 1 < chunks)
        def _():
            tokens_in(k + members - 1, 0, (k + members - 1) % members).start()

        @pl.when(k == (2 * chunks) // 3)
        def _():
            relay(0)

        tokens_in(k, 0, slot_x).wait()
        for f in range(nf):
            g = k * nf + f
            slot = g % depth
            weights(g, slot, False)
            weights(g + depth - 1, (g + depth - 1) % depth, True)

            @pl.when(k == 0)
            def _():
                acc_g[f] = dot(xbuf[slot_x], wbuf[slot, 0])
                acc_u[f] = dot(xbuf[slot_x], wbuf[slot, 1])

            @pl.when(k > 0)
            def _():
                acc_g[f] += dot(xbuf[slot_x], wbuf[slot, 0])
                acc_u[f] += dot(xbuf[slot_x], wbuf[slot, 1])

    for f in range(nf):
        activate(None, f, 0, hs, False, False)

    for i in range(members - 1):
        tell(i).wait_recv()
    for r in range(members):
        at = (meta if r == 0 else mbuf.at[r - 1])[:top, :] - (me * local * slots).astype(F32)

        @pl.loop(0, local)
        def _(e):
            row = (lax.broadcasted_iota(jnp.int32, (slots, tokens), 0) + e * slots).astype(F32)
            hit = at[0:1] == row
            for j in range(1, top):
                hit |= at[j : j + 1] == row
            onehot[r, block(e, slots), :] = jnp.where(hit, 1.0, 0.0).astype(BF16)

    for side in range(2):
        second(jnp.int32(0), side).wait_recv()
    for r in range(members):
        tokens_in(0, r, r).start()

    @pl.loop(0, chunks)
    def _(k):
        for r in range(members):
            tokens_in(k, r, r).wait()
        for r in range(members):
            for j in range(2):
                n = local // 2
                v = dot(onehot[r, pl.ds(j * n * slots, n * slots), :], xbuf[r]).astype(BF16)
                z[j * n : (j + 1) * n, r * slots : (r + 1) * slots, :] = v.reshape(n, slots, width)

        @pl.loop(0, steps)
        def _(i):
            g = head + k * steps + i
            slot = g % depth

            @pl.when((i == (2 * steps) // 5) & (k + 1 < chunks))
            def _():
                relay(k + 1)

            @pl.when((i == (4 * steps) // 5) & (k + 1 < chunks))
            def _():
                for side in range(2):
                    second(k + 1, side).wait_recv()
                for r in range(members):
                    tokens_in(k + 1, r, r).start()

            weights(g, slot, False)
            weights(g + depth - 1, (g + depth - 1) % depth, True)
            e = i // nf

            @pl.when(k == 0)
            def _():
                acc_g[i] = dot(z[e], wbuf[slot, 0])
                acc_u[i] = dot(z[e], wbuf[slot, 1])

            @pl.when((k > 0) & (k < chunks - 1))
            def _():
                acc_g[i] += dot(z[e], wbuf[slot, 0])
                acc_u[i] += dot(z[e], wbuf[slot, 1])

            @pl.when(k == chunks - 1)
            def _():
                activate(z[e], i, slot, h.at[e], True, True)

    for p in range(ff // hw):
        put(hs.at[:, pl.ds(0, hw)], p).wait()
    for i in range(members - 1):
        tell(i).wait_send()

    @pl.loop(0, chunks)
    def _(k):
        for side in range(2):
            first(k, side).wait_send()
            second(k, side).wait_send()

    metas[0] = meta[...]
    metas[1:] = mbuf[...]


def scatter_kernel(
    members, h, hs, metas, w_down, s_down, y,
    hbuf, comb, wbuf, outs, pend, own, abuf, bbuf, arecv, brecv, ybuf,
    hsem, wsem, a_s, a_r, b_s, b_r, ysem,
):
    (local, rows, ff), width, d = h.shape, wbuf.shape[3], y.shape[1]
    tokens, top = hs.shape[0], metas.shape[2] // 2
    slots, half, chunks = rows // members, tokens // 2, d // width
    depth, pairs, lag = wbuf.shape[0], local // 2, own.shape[0] - 1
    steps = pairs + 1
    me, right, left, _ = ring(members)
    sides = (right, left)
    greet(right, left)

    def weights(g, slot, start):
        n, p = g // steps, g % steps

        def go(copy):
            copy.start() if start else copy.wait()

        @pl.when((p < pairs) & (n < chunks))
        def _():
            for i in range(2):
                go(pltpu.make_async_copy(w_down.at[2 * p + i, :, block(n, width)], wbuf.at[slot, i], wsem.at[slot, i]))

        @pl.when((p == pairs) & (n < chunks))
        def _():
            go(pltpu.make_async_copy(s_down.at[:, block(n, width)], wbuf.at[slot, 0], wsem.at[slot, 0]))

    def take(e):
        return pltpu.make_async_copy(h.at[e], hbuf.at[e], hsem.at[e])

    def across(n, side):
        return remote(abuf.at[n % 2, pl.ds(side * half, half)], arecv.at[n, side], a_s.at[n, side], a_r.at[n, side], sides[side])

    def beside(n, side):
        return remote(bbuf.at[n % 2, side], brecv.at[n, side], b_s.at[n, side], b_r.at[n, side], sides[side])

    def put(n):
        return pltpu.make_async_copy(ybuf.at[n % 2], y.at[:, block(n, width)], ysem.at[n % 2])

    for e in range(local):
        take(e).start()
    for g in range(depth - 1):
        weights(jnp.int32(g), g, True)

    base = (me * local * slots).astype(F32)
    for r in range(members):

        @pl.loop(0, tokens // 96)
        def _(t):
            part = block(t, 96)
            at, gate = metas[r, part, :top] - base, metas[r, part, top:]
            row = lax.broadcasted_iota(jnp.int32, (96, local * slots), 1).astype(F32)
            v = jnp.zeros(row.shape, F32)
            for j in range(top):
                v = jnp.where(at[:, j : j + 1] == row, gate[:, j : j + 1], v)
            comb[r, part, :] = v.astype(BF16)

    def pair(n, p):
        g = n * steps + p
        slot = g % depth

        @pl.when(n == 0)
        def _():
            for i in range(2):
                take(2 * p + i).wait()

        weights(g, slot, False)
        weights(g + depth - 1, (g + depth - 1) % depth, True)
        for i in range(2):
            v = dot(hbuf[2 * p + i], wbuf[slot, i]).astype(BF16)
            outs[:, 2 * p + i] = v.reshape(members, slots, width)

    @pl.loop(0, chunks + lag)
    def _(n):
        @pl.when(n < chunks)
        def _():
            @pl.loop(0, (pairs + 1) // 2)
            def _(p):
                pair(n, p)

        @pl.when((n >= 1) & (n <= chunks))
        def _():
            m = n - 1
            for side in range(2):
                across(m, side).wait_recv()
            for side in range(2):

                @pl.when(m >= 2)
                def _():
                    beside(m - 2, side).wait_send()

                mine, other = pl.ds(side * half, half), pl.ds((1 - side) * half, half)
                v = pend[m % 2, side, mine] + arecv[m, side].astype(F32)
                bbuf[m % 2, side, mine] = v.astype(BF16)
                bbuf[m % 2, side, other] = pend[m % 2, side, other].astype(BF16)
                beside(m, side).start()

        @pl.when(n < chunks)
        def _():
            @pl.loop((pairs + 1) // 2, pairs)
            def _(p):
                pair(n, p)

            def term(r):
                return dot(comb[r], outs[r].reshape(local * slots, width))

            @pl.when(n >= 2)
            def _():
                for side in range(2):
                    across(n - 2, side).wait_send()

            abuf[n % 2] = term(3).astype(BF16)
            for side in range(2):
                across(n, side).start()
            g = n * steps + pairs
            slot = g % depth
            weights(g, slot, False)
            weights(g + depth - 1, (g + depth - 1) % depth, True)
            pend[n % 2, 0] = term(2)
            pend[n % 2, 1] = term(1)
            own[n % (lag + 1)] = term(0) + dot(hs[...], wbuf[slot, 0])

        @pl.when(n >= lag)
        def _():
            q = n - lag
            for side in range(2):
                beside(q, side).wait_recv()

            @pl.when(q >= 2)
            def _():
                put(q - 2).wait()

            ybuf[q % 2] = (own[q % (lag + 1)] + brecv[q, 0].astype(F32) + brecv[q, 1].astype(F32)).astype(BF16)
            put(q).start()

    for n in range(chunks - 2, chunks):
        put(jnp.int32(n)).wait()
        for side in range(2):
            across(jnp.int32(n), side).wait_send()
            beside(jnp.int32(n), side).wait_send()


def gather(members, x, meta, w_gate, w_up, s_gate, s_up, slots):
    (tokens, d), (local, _, ff) = x.shape, w_gate.shape
    rows, chunks, hw = members * slots, d // X_COLUMNS, ff // 2
    steps = local * ff // F_COLUMNS
    hbm, vmem = pl.BlockSpec(memory_space=pl.ANY), pl.BlockSpec(memory_space=pltpu.VMEM)
    dma = pltpu.SemaphoreType.DMA
    return pl.pallas_call(
        lambda *refs: gather_kernel(members, *refs),
        name="gather_project",
        out_shape=(
            jax.ShapeDtypeStruct((local, rows, ff), BF16),
            jax.ShapeDtypeStruct((tokens, ff), BF16),
            jax.ShapeDtypeStruct((members - 1, tokens, d), BF16),
            jax.ShapeDtypeStruct((members, *meta.shape), F32),
        ),
        in_specs=[hbm, vmem, hbm, hbm, hbm, hbm],
        out_specs=(hbm, hbm, hbm, vmem),
        scratch_shapes=[
            pltpu.VMEM((steps, rows, F_COLUMNS), F32),
            pltpu.VMEM((steps, rows, F_COLUMNS), F32),
            pltpu.VMEM((members, tokens, X_COLUMNS), BF16),
            pltpu.VMEM((local, rows, X_COLUMNS), BF16),
            pltpu.VMEM((members, local * slots, tokens), BF16),
            pltpu.VMEM((X_RING, 2, X_COLUMNS, F_COLUMNS), BF16),
            pltpu.VMEM((ff // hw, rows, hw), BF16),
            pltpu.VMEM((members - 1, *meta.shape), F32),
            dma((chunks, 2)), dma((chunks, 2)), dma((chunks, 2)), dma((chunks, 2)),
            dma((members - 1,)), dma((members - 1,)), dma((X_RING, 2)), dma((members,)), dma((ff // hw,)),
        ],
        compiler_params=pltpu.CompilerParams(collective_id=0, has_side_effects=True, vmem_limit_bytes=VMEM_BYTES),
    )(x, meta, w_gate, w_up, s_gate, s_up)


def scatter(members, h, hs, metas, w_down, s_down):
    (local, rows, ff), (tokens, d) = h.shape, (hs.shape[0], w_down.shape[2])
    chunks, half = d // Y_COLUMNS, tokens // 2
    slots = rows // members
    hbm, vmem = pl.BlockSpec(memory_space=pl.ANY), pl.BlockSpec(memory_space=pltpu.VMEM)
    dma = pltpu.SemaphoreType.DMA
    return pl.pallas_call(
        lambda *refs: scatter_kernel(members, *refs),
        name="project_scatter",
        out_shape=jax.ShapeDtypeStruct((tokens, d), BF16),
        in_specs=[hbm, vmem, vmem, hbm, hbm],
        out_specs=hbm,
        scratch_shapes=[
            pltpu.VMEM(h.shape, BF16),
            pltpu.VMEM((members, tokens, local * slots), BF16),
            pltpu.VMEM((Y_RING, 2, ff, Y_COLUMNS), BF16),
            pltpu.VMEM((members, local, slots, Y_COLUMNS), BF16),
            pltpu.VMEM((2, 2, tokens, Y_COLUMNS), F32),
            pltpu.VMEM((LAG + 1, tokens, Y_COLUMNS), F32),
            pltpu.VMEM((2, tokens, Y_COLUMNS), BF16),
            pltpu.VMEM((2, 2, tokens, Y_COLUMNS), BF16),
            pltpu.VMEM((chunks, 2, half, Y_COLUMNS), BF16),
            pltpu.VMEM((chunks, 2, tokens, Y_COLUMNS), BF16),
            pltpu.VMEM((2, tokens, Y_COLUMNS), BF16),
            dma((local,)), dma((Y_RING, 2)),
            dma((chunks, 2)), dma((chunks, 2)), dma((chunks, 2)), dma((chunks, 2)), dma((2,)),
        ],
        compiler_params=pltpu.CompilerParams(collective_id=1, has_side_effects=True, vmem_limit_bytes=VMEM_BYTES),
    )(h, hs, metas, w_down, s_down)


def solution(mesh):
    members = mesh.shape["ep"]

    def body(x, expert, slot, gate, w_gate, w_up, w_down, s_gate, s_up, s_down):
        x, expert, slot, gate = (v[0, 0] for v in (x, expert, slot, gate))
        tokens, top = expert.shape
        slots = 5 * tokens * top // (4 * w_gate.shape[0] * members)
        at = jnp.where(slot < slots, expert * slots + slot, -1).astype(F32)
        meta = jnp.concatenate([at, gate.astype(BF16).astype(F32)], 1).T
        h, hs, _, metas = gather(members, x, meta, w_gate, w_up, s_gate, s_up, slots)
        y = scatter(members, h, hs, metas.transpose(0, 2, 1), w_down, s_down)
        return y[None, None]

    tok, exp, rep = P("dp", "ep"), P("ep"), P()
    return jax.shard_map(
        body,
        mesh=mesh,
        in_specs=(tok,) * 4 + (exp,) * 3 + (rep,) * 3,
        out_specs=tok,
        check_vma=False,
    )
```

time: 1210 us -> 406 us (0.34)
  blocking collectives: 447 us -> 0 us
  Pallas kernels: 0 us -> 397 us
  waiting for transfers between devices: 381 us -> 0 us
  matrix products: 342 us -> 0 us
  local copies, waits for them, and re-layouts: 28.6 us -> 6.33 us
    another operation x1 -> x0, blocking collectives: 447 us -> none  [placed(): return lax.with_sharding_constraint(v, NamedSharding(mesh, P(*spec)))]
    pallas_call x0 -> x2, Pallas kernels: none -> 397 us  [the longest x1 243 us: gather(): pl.pallas_call(lambda *refs: gather_kernel(members, *refs), name='gather_...]
    another operation x1 -> x0, waiting for transfers between devices: 381 us -> none  [placed(): return lax.with_sharding_constraint(v, NamedSharding(mesh, P(*spec)))]
    dot_general x9 -> x0, matrix products: 342 us -> none  [einsum(): return jnp.einsum(form, a.astype(jnp.float32), b.astype(jnp.float32))]
    another operation x1 -> x0, local copies, waits for them, and re-layouts: 26.7 us -> none  [placed(): return lax.with_sharding_constraint(v, NamedSharding(mesh, P(*spec)))]
  transfers between devices with their start and end apart: 1 -> 0, of which waited for: 1 -> 0; matrix products, arithmetic and copies ran while one was open for 4% -> 0% of each run, Pallas kernels for 0% -> 0%
where the time goes in v1:
time: 406 us; the launch traced here: 405 us
  Pallas kernels  397 us (98%)
  local copies, waits for them, and re-layouts  6.33 us (2%)
    pallas_call x1, Pallas kernels, gather(): pl.pallas_call(lambda *refs: gather_kernel(members, *refs), name='gather_...  243 us
    pallas_call x1, Pallas kernels, scatter(): pl.pallas_call(lambda *refs: scatter_kernel(members, *refs), name='projec...  154 us

profile of v1, /device:TPU:112, one launch (start us, length us, event | category | flops | bytes accessed | tf_op | source)
XLA Modules:
  0.0 405.1 jit_solution(12011309764051303224)
XLA Ops:
  0.0 0.7 convert_bitcast_fusion
  0.7 0.7 bitcast_convert_fusion
  1.4 0.6 maximum_bitcast_fusion.refs_1_
  2.1 242.9 %gather_project.1 = (bf16[10,384,1536]{2,1,0:T(8,128)(2,1)}, bf16[384,1536]{1,0:T(8,128)(2,1)}, bf16[3,384,5120]{2,1,0:T(8,128)(2,1)}, f32[4,16,384]{2,1,0:T(8,128)}) custom-call(bf16[384,5120]{1,0:T(8,128)(2,1)} %bitcast.11, f32[16,384]{1,0:T(8,128)} %maximum_bitcast_fusion.refs_1_, bf16[10,5120,1536]{2,1,0:T(8,128)(2,1)} %refs_2_.1, ...), custom_call_target="tpu_custom_call" | custom-call | tf_op jit(solution)/shard_map/gather_project/pallas_call | solution.py:387
  245.0 2.0 copy.11
  247.0 153.8 %project_scatter.1 = bf16[384,5120]{1,0:T(8,128)(2,1)} custom-call(bf16[10,384,1536]{2,1,0:T(8,128)(2,1)} %get-tuple-element.8.refs_0_, bf16[384,1536]{1,0:T(8,128)(2,1)} %get-tuple-element.9.refs_1_, f32[4,384,16]{2,1,0:T(8,128)} %bitcast.12, bf16[10,1536,5120]{2,1,0:T(8,128)(2,1)} %refs_3_.3, bf16[1536,5120]{1,0:T(8,128)(2,1)} %refs_4_.3), custom_call_target="tpu_custom_call" | custom-call | tf_op jit(solution)/shard_map/project_scatter/pallas_call | solution.py:420
  400.8 4.3 %copy.13 = bf16[1,1,384,5120]{3,2,1,0:T(8,128)(2,1)} copy(bf16[1,1,384,5120]{3,2,1,0:T(8,128)(2,1)} %bitcast.10) | data formatting | bytes 7864320

commit v2 on v1

v2 whole, which is shorter than its diff:
```python
import jax
import jax.numpy as jnp
from jax import lax
from jax.experimental import pallas as pl
from jax.experimental.pallas import tpu as pltpu
from jax.sharding import PartitionSpec as P

F32, BF16 = jnp.float32, jnp.bfloat16
MESH = pl.DeviceIdType.MESH
VMEM_BYTES = 67_000_000
X_COLUMNS, F_COLUMNS, H_COLUMNS, H_RING, X_RING = 512, 1536, 256, 4, 3
Y_COLUMNS, Y_GROUP, Y_RING, LAG, MARK_ROWS = 256, 5, 3, 3, 16


def dot(a, b):
    return jnp.dot(a, b, preferred_element_type=F32)


def ring(members):
    me = lax.axis_index("ep")
    return me, lax.rem(me + 1, members), lax.rem(me + members - 1, members), lax.rem(me + 2, members)


def greet(*devices):
    barrier = pltpu.get_barrier_semaphore()
    for device in devices:
        pl.semaphore_signal(barrier, inc=1, device_id={"ep": device}, device_id_type=MESH)
    pl.semaphore_wait(barrier, len(devices))


def remote(src, dst, send, recv, device):
    return pltpu.make_async_remote_copy(
        src_ref=src, dst_ref=dst, send_sem=send, recv_sem=recv, device_id={"ep": device}, device_id_type=MESH
    )


def block(i, size):
    return pl.ds(pl.multiple_of(i * size, size), size)


def gather_kernel(
    members, x, expert, slot, gate, w_gate, w_up, s_gate, s_up, h, hs, xg, metas,
    acc_g, acc_u, xbuf, z, onehot, wbuf, hbuf, mbuf,
    s1s, s1r, s2s, s2r, ms, mr, wsem, xsem, hsem,
):
    (tokens, d), local, (_, rows, width) = x.shape, w_gate.shape[0], z.shape
    slots, half, chunks = rows // members, tokens // 2, d // width
    depth, fb = wbuf.shape[0], wbuf.shape[3]
    ff, hw, top = w_gate.shape[2], hbuf.shape[2], expert.shape[0]
    nf = ff // fb
    head, steps = chunks * nf, local * nf
    me, right, left, across = ring(members)
    sides = (right, left)
    mbuf[0, :top] = jnp.where(slot[...] < slots, expert[...] * slots + slot[...], -1).astype(F32)
    mbuf[0, top:] = gate[...].astype(BF16).astype(F32)
    greet(right, left, across)

    def first(k, side):
        return remote(x.at[:, block(k, width)], xg.at[side, :, block(k, width)], s1s.at[k, side], s1r.at[k, side], sides[side])

    def second(k, side):
        part = pl.ds(side * half, half)
        return remote(
            xg.at[side, part, block(k, width)], xg.at[2, part, block(k, width)], s2s.at[k, side], s2r.at[k, side], sides[side]
        )

    def tell(i):
        return remote(mbuf.at[0], mbuf.at[i + 1], ms.at[i], mr.at[i], (right, left, across)[i])

    def relay(k):
        for side in range(2):
            first(k, side).wait_recv()
        for side in range(2):
            second(k, side).start()

        @pl.when(k + 1 < chunks)
        def _():
            for side in range(2):
                first(k + 1, side).start()

    def weights(g, slot, start):
        def copies(gate, up):
            for i, src in enumerate((gate, up)):
                copy = pltpu.make_async_copy(src, wbuf.at[slot, i], wsem.at[slot, i])
                copy.start() if start else copy.wait()

        if not start:
            return copies(s_gate.at[:width, :fb], s_up.at[:width, :fb])

        @pl.when(g < head)
        def _():
            k, f = g // nf, g % nf
            copies(*(s.at[block(k, width), block(f, fb)] for s in (s_gate, s_up)))

        @pl.when((g >= head) & (g < head + chunks * steps))
        def _():
            k, i = (g - head) // steps, (g - head) % steps
            copies(*(w.at[i // nf, block(k, width), block(i % nf, fb)] for w in (w_gate, w_up)))

    def tokens_in(k, source, slot):
        src = x if source == 0 else xg.at[source - 1]
        return pltpu.make_async_copy(src.at[:, block(k, width)], xbuf.at[slot], xsem.at[slot])

    def put(dst, p):
        return pltpu.make_async_copy(hbuf.at[p], dst, hsem.at[p])

    def activate(zz, i, slot, dst, last):
        for j in range(fb // hw):
            part = pl.ds(j * hw, hw)
            g, u = acc_g[i, :, part], acc_u[i, :, part]
            if last:
                g += dot(zz, wbuf[slot, 0, :, part])
                u += dot(zz, wbuf[slot, 1, :, part])
            v = (jax.nn.silu(g) * u).astype(BF16)
            p = (i % nf) * (fb // hw) + j
            c = (i + nf if last else i) * (fb // hw) + j
            if last or c >= H_RING:
                put(hs.at[:, pl.ds(0, hw)], c % H_RING).wait()
            hbuf[c % H_RING] = v
            put(dst.at[:, block(p, hw)], c % H_RING).start()

    def mark(r):
        at = mbuf[r, :top] - (me * local * slots).astype(F32)
        for e in range(local):
            row = (lax.broadcasted_iota(jnp.int32, (slots, tokens), 0) + e * slots).astype(F32)
            hit = at[0:1] == row
            for j in range(1, top):
                hit |= at[j : j + 1] == row
            n = e % (local // 2) * slots
            onehot[r, e // (local // 2), n : n + slots, :] = jnp.where(hit, 1.0, 0.0).astype(BF16)

    for side in range(2):
        first(0, side).start()
    for k in range(members - 1):
        tokens_in(k, 0, k).start()
    for g in range(depth - 1):
        weights(jnp.int32(g), g, True)
    for i in range(members - 1):
        tell(i).start()

    @pl.loop(0, chunks)
    def _(k):
        slot_x = k % members

        @pl.when(k + members - 1 < chunks)
        def _():
            tokens_in(k + members - 1, 0, (k + members - 1) % members).start()

        @pl.when(k == (2 * chunks) // 3)
        def _():
            relay(0)

        @pl.when(k == chunks - members)
        def _():
            for i in range(members - 1):
                tell(i).wait_recv()

        tokens_in(k, 0, slot_x).wait()
        for f in range(nf):
            g = k * nf + f
            slot = g % depth
            weights(g, slot, False)
            weights(g + depth - 1, (g + depth - 1) % depth, True)

            @pl.when(k == 0)
            def _():
                acc_g[f] = dot(xbuf[slot_x], wbuf[slot, 0])
                acc_u[f] = dot(xbuf[slot_x], wbuf[slot, 1])

            @pl.when((k > 0) & (k < chunks - members))
            def _():
                acc_g[f] += dot(xbuf[slot_x], wbuf[slot, 0])
                acc_u[f] += dot(xbuf[slot_x], wbuf[slot, 1])

            @pl.when(k >= chunks - members)
            def _():
                if f == 0:
                    mark(k - (chunks - members))
                acc_g[f] += dot(xbuf[slot_x], wbuf[slot, 0])
                acc_u[f] += dot(xbuf[slot_x], wbuf[slot, 1])

    for f in range(nf):
        activate(None, f, 0, hs, False)

    for side in range(2):
        second(jnp.int32(0), side).wait_recv()
    for r in range(members):
        tokens_in(0, r, r).start()

    @pl.loop(0, 2 * chunks)
    def _(t):
        k, j = t // 2, t % 2

        @pl.when(j == 0)
        def _():
            for r in range(members):
                tokens_in(k, r, r).wait()

        for r in range(members):
            v = dot(onehot[r, j], xbuf[r]).astype(BF16)
            z[:, r * slots : (r + 1) * slots, :] = v.reshape(local // 2, slots, width)

        @pl.loop(0, steps // 2)
        def _(s):
            i = j * (steps // 2) + s
            g = head + k * steps + i
            slot = g % depth

            @pl.when((i == steps // 5) & (k + 1 < chunks))
            def _():
                relay(k + 1)

            @pl.when((i == (4 * steps) // 5) & (k + 1 < chunks))
            def _():
                for side in range(2):
                    second(k + 1, side).wait_recv()
                for r in range(members):
                    tokens_in(k + 1, r, r).start()

            weights(g, slot, False)
            weights(g + depth - 1, (g + depth - 1) % depth, True)
            e = s // nf

            @pl.when(k == 0)
            def _():
                acc_g[i] = dot(z[e], wbuf[slot, 0])
                acc_u[i] = dot(z[e], wbuf[slot, 1])

            @pl.when((k > 0) & (k < chunks - 1))
            def _():
                acc_g[i] += dot(z[e], wbuf[slot, 0])
                acc_u[i] += dot(z[e], wbuf[slot, 1])

            @pl.when(k == chunks - 1)
            def _():
                activate(z[e], i, slot, h.at[i // nf], True)

    for p in range(H_RING):
        put(hs.at[:, pl.ds(0, hw)], p).wait()
    for i in range(members - 1):
        tell(i).wait_send()

    @pl.loop(0, chunks)
    def _(k):
        for side in range(2):
            first(k, side).wait_send()
            second(k, side).wait_send()

    metas[...] = mbuf[...]


def scatter_kernel(
    members, h, hs, metas, w_down, s_down, y,
    hbuf, comb, wbuf, outs, pend, own, abuf, bbuf, arecv, brecv, ybuf,
    hsem, wsem, a_s, a_r, b_s, b_r, ysem,
):
    (local, rows, ff), width, d = h.shape, wbuf.shape[3], y.shape[1]
    tokens, top = hs.shape[0], metas.shape[1] // 2
    slots, half, chunks = rows // members, tokens // 2, d // width
    (depth, group), lag = wbuf.shape[:2], own.shape[0] - 1
    groups = local // group
    steps = groups + 1
    me, right, left, _ = ring(members)
    sides = (right, left)
    greet(right, left)

    def weights(g, slot, start):
        n, p = g // steps, g % steps

        def go(copy):
            copy.start() if start else copy.wait()

        @pl.when((p < groups) & (n < chunks))
        def _():
            for i in range(group):
                go(pltpu.make_async_copy(w_down.at[group * p + i, :, block(n, width)], wbuf.at[slot, i], wsem.at[slot, i]))

        @pl.when((p == groups) & (n < chunks))
        def _():
            go(pltpu.make_async_copy(s_down.at[:, block(n, width)], wbuf.at[slot, 0], wsem.at[slot, 0]))

    def take(e):
        return pltpu.make_async_copy(h.at[e], hbuf.at[e], hsem.at[e])

    def across(n, side):
        return remote(abuf.at[n % 2, pl.ds(side * half, half)], arecv.at[n, side], a_s.at[n, side], a_r.at[n, side], sides[side])

    def beside(n, side):
        return remote(bbuf.at[n % 2, side], brecv.at[n, side], b_s.at[n, side], b_r.at[n, side], sides[side])

    def put(n):
        return pltpu.make_async_copy(ybuf.at[n % 2], y.at[:, block(n, width)], ysem.at[n % 2])

    for e in range(local):
        take(e).start()
    for g in range(depth - 1):
        weights(jnp.int32(g), g, True)

    def mark(r):
        m = metas[r].T
        at, gate = m[:, :top] - (me * local * slots).astype(F32), m[:, top:]
        row = lax.broadcasted_iota(jnp.int32, (MARK_ROWS, local * slots), 1).astype(F32)
        for t in range(0, tokens, MARK_ROWS):
            v = jnp.zeros(row.shape, F32)
            for j in range(top):
                v = jnp.where(at[t : t + MARK_ROWS, j : j + 1] == row, gate[t : t + MARK_ROWS, j : j + 1], v)
            comb[r, t : t + MARK_ROWS] = v.astype(BF16)

    mark(3)
    mark(2)

    @pl.loop(0, chunks + lag)
    def _(n):
        @pl.when(n < chunks)
        def _():
            @pl.loop(0, groups)
            def _(p):
                g = n * steps + p
                slot = g % depth

                @pl.when(n == 0)
                def _():
                    for i in range(group):
                        take(group * p + i).wait()

                weights(g, slot, False)
                weights(g + depth - 1, (g + depth - 1) % depth, True)
                for i in range(group):
                    v = dot(hbuf[group * p + i], wbuf[slot, i]).astype(BF16)
                    outs[:, group * p + i] = v.reshape(members, slots, width)

            def term(r):
                return dot(comb[r], outs[r].reshape(local * slots, width))

            @pl.when(n >= 2)
            def _():
                for side in range(2):
                    across(n - 2, side).wait_send()

            abuf[n % 2] = term(3).astype(BF16)
            for side in range(2):
                across(n, side).start()

            @pl.when(n == 0)
            def _():
                mark(1)
                mark(0)

            g = n * steps + groups
            slot = g % depth
            weights(g, slot, False)
            weights(g + depth - 1, (g + depth - 1) % depth, True)
            pend[n % 2, 0] = term(2)
            pend[n % 2, 1] = term(1)
            own[n % (lag + 1)] = term(0) + dot(hs[...], wbuf[slot, 0])

        @pl.when((n >= 1) & (n <= chunks))
        def _():
            m = n - 1
            for side in range(2):
                across(m, side).wait_recv()

            @pl.when(m >= 2)
            def _():
                for side in range(2):
                    beside(m - 2, side).wait_send()

            for side in range(2):
                mine, other = pl.ds(side * half, half), pl.ds((1 - side) * half, half)
                v = pend[m % 2, side, mine] + arecv[m, side].astype(F32)
                bbuf[m % 2, side, mine] = v.astype(BF16)
                bbuf[m % 2, side, other] = pend[m % 2, side, other].astype(BF16)
                beside(m, side).start()

        @pl.when(n >= lag)
        def _():
            q = n - lag
            for side in range(2):
                beside(q, side).wait_recv()

            @pl.when(q >= 2)
            def _():
                put(q - 2).wait()

            ybuf[q % 2] = (own[q % (lag + 1)] + brecv[q, 0].astype(F32) + brecv[q, 1].astype(F32)).astype(BF16)
            put(q).start()

    for n in range(chunks - 2, chunks):
        put(jnp.int32(n)).wait()
        for side in range(2):
            across(jnp.int32(n), side).wait_send()
            beside(jnp.int32(n), side).wait_send()


def gather(members, x, expert, slot, gate, w_gate, w_up, s_gate, s_up, slots):
    (tokens, d), (local, _, ff) = x.shape, w_gate.shape
    rows, chunks, hw, top = members * slots, d // X_COLUMNS, H_COLUMNS, expert.shape[0]
    steps = local * ff // F_COLUMNS
    hbm, vmem = pl.BlockSpec(memory_space=pl.ANY), pl.BlockSpec(memory_space=pltpu.VMEM)
    dma = pltpu.SemaphoreType.DMA
    return pl.pallas_call(
        lambda *refs: gather_kernel(members, *refs),
        name="gather_project",
        out_shape=(
            jax.ShapeDtypeStruct((local, rows, ff), BF16),
            jax.ShapeDtypeStruct((tokens, ff), BF16),
            jax.ShapeDtypeStruct((members - 1, tokens, d), BF16),
            jax.ShapeDtypeStruct((members, 2 * top, tokens), F32),
        ),
        in_specs=[hbm, vmem, vmem, vmem, hbm, hbm, hbm, hbm],
        out_specs=(hbm, hbm, hbm, vmem),
        scratch_shapes=[
            pltpu.VMEM((steps, rows, F_COLUMNS), F32),
            pltpu.VMEM((steps, rows, F_COLUMNS), F32),
            pltpu.VMEM((members, tokens, X_COLUMNS), BF16),
            pltpu.VMEM((local // 2, rows, X_COLUMNS), BF16),
            pltpu.VMEM((members, 2, local // 2 * slots, tokens), BF16),
            pltpu.VMEM((X_RING, 2, X_COLUMNS, F_COLUMNS), BF16),
            pltpu.VMEM((H_RING, rows, hw), BF16),
            pltpu.VMEM((members, 2 * top, tokens), F32),
            dma((chunks, 2)), dma((chunks, 2)), dma((chunks, 2)), dma((chunks, 2)),
            dma((members - 1,)), dma((members - 1,)), dma((X_RING, 2)), dma((members,)), dma((H_RING,)),
        ],
        compiler_params=pltpu.CompilerParams(collective_id=0, has_side_effects=True, vmem_limit_bytes=VMEM_BYTES),
    )(x, expert, slot, gate, w_gate, w_up, s_gate, s_up)


def scatter(members, h, hs, metas, w_down, s_down):
    (local, rows, ff), (tokens, d) = h.shape, (hs.shape[0], w_down.shape[2])
    chunks, half = d // Y_COLUMNS, tokens // 2
    slots = rows // members
    hbm, vmem = pl.BlockSpec(memory_space=pl.ANY), pl.BlockSpec(memory_space=pltpu.VMEM)
    dma = pltpu.SemaphoreType.DMA
    return pl.pallas_call(
        lambda *refs: scatter_kernel(members, *refs),
        name="project_scatter",
        out_shape=jax.ShapeDtypeStruct((tokens, d), BF16),
        in_specs=[hbm, vmem, vmem, hbm, hbm],
        out_specs=hbm,
        scratch_shapes=[
            pltpu.VMEM(h.shape, BF16),
            pltpu.VMEM((members, tokens, local * slots), BF16),
            pltpu.VMEM((Y_RING, Y_GROUP, ff, Y_COLUMNS), BF16),
            pltpu.VMEM((members, local, slots, Y_COLUMNS), BF16),
            pltpu.VMEM((2, 2, tokens, Y_COLUMNS), F32),
            pltpu.VMEM((LAG + 1, tokens, Y_COLUMNS), F32),
            pltpu.VMEM((2, tokens, Y_COLUMNS), BF16),
            pltpu.VMEM((2, 2, tokens, Y_COLUMNS), BF16),
            pltpu.VMEM((chunks, 2, half, Y_COLUMNS), BF16),
            pltpu.VMEM((chunks, 2, tokens, Y_COLUMNS), BF16),
            pltpu.VMEM((2, tokens, Y_COLUMNS), BF16),
            dma((local,)), dma((Y_RING, Y_GROUP)),
            dma((chunks, 2)), dma((chunks, 2)), dma((chunks, 2)), dma((chunks, 2)), dma((2,)),
        ],
        compiler_params=pltpu.CompilerParams(collective_id=1, has_side_effects=True, vmem_limit_bytes=VMEM_BYTES),
    )(h, hs, metas, w_down, s_down)


def solution(mesh):
    members = mesh.shape["ep"]

    def body(x, expert, slot, gate, w_gate, w_up, w_down, s_gate, s_up, s_down):
        x, expert, slot, gate = (v[0, 0] for v in (x, expert, slot, gate))
        tokens, top = expert.shape
        slots = 5 * tokens * top // (4 * w_gate.shape[0] * members)
        h, hs, _, metas = gather(members, x, expert.T, slot.T, gate.T, w_gate, w_up, s_gate, s_up, slots)
        y = scatter(members, h, hs, metas, w_down, s_down)
        return y[None, None]

    tok, exp, rep = P("dp", "ep"), P("ep"), P()
    return jax.shard_map(
        body,
        mesh=mesh,
        in_specs=(tok,) * 4 + (exp,) * 3 + (rep,) * 3,
        out_specs=tok,
        check_vma=False,
    )
```

time: 406 us -> 362 us (0.89)
  Pallas kernels: 397 us -> 358 us
    pallas_call x1, Pallas kernels: 243 us -> 209 us  [gather(): pl.pallas_call(lambda *refs: gather_kernel(members, *refs), name='gather_...]
    pallas_call x1, Pallas kernels: 154 us -> 148 us  [scatter(): pl.pallas_call(lambda *refs: scatter_kernel(members, *refs), name='projec...]
where the time goes in v2:
time: 362 us
  Pallas kernels  358 us (99%)
  local copies, waits for them, and re-layouts  4.29 us (1%)
    pallas_call x1, Pallas kernels, gather(): pl.pallas_call(lambda *refs: gather_kernel(members, *refs), name='gather_...  209 us
    pallas_call x1, Pallas kernels, scatter(): pl.pallas_call(lambda *refs: scatter_kernel(members, *refs), name='projec...  148 us

profile of v2, /device:TPU:112, one launch (start us, length us, event | category | flops | bytes accessed | tf_op | source)
XLA Modules:
  0.0 361.9 jit_solution(2115562886343741510)
XLA Ops:
  0.0 209.4 %gather_project.1 = (bf16[10,384,1536]{2,1,0:T(8,128)(2,1)}, bf16[384,1536]{1,0:T(8,128)(2,1)}, bf16[3,384,5120]{2,1,0:T(8,128)(2,1)}, f32[4,16,384]{2,1,0:T(8,128)}) custom-call(bf16[384,5120]{1,0:T(8,128)(2,1)} %bitcast.12, s32[8,384]{1,0:T(8,128)} %bitcast.13, s32[8,384]{1,0:T(8,128)} %bitcast.14, f32[8,384]{1,0:T(8,128)} %bitcast.15, ...), custom_call_target="tpu_custom_call" | custom-call | tf_op jit(solution)/shard_map/gather_project/pallas_call | solution.py:401
  209.4 148.1 %project_scatter.1 = bf16[384,5120]{1,0:T(8,128)(2,1)} custom-call(bf16[10,384,1536]{2,1,0:T(8,128)(2,1)} %get-tuple-element.8.refs_0_, bf16[384,1536]{1,0:T(8,128)(2,1)} %get-tuple-element.9.refs_1_, f32[4,16,384]{2,1,0:T(8,128)} %get-tuple-element.10.refs_2_, bf16[10,1536,5120]{2,1,0:T(8,128)(2,1)} %refs_3_.1, bf16[1536,5120]{1,0:T(8,128)(2,1)} %refs_4_.3), custom_call_target="tpu_custom_call" | custom-call | tf_op jit(solution)/shard_map/project_scatter/pallas_call | solution.py:434
  357.6 4.3 %copy.12 = bf16[1,1,384,5120]{3,2,1,0:T(8,128)(2,1)} copy(bf16[1,1,384,5120]{3,2,1,0:T(8,128)(2,1)} %bitcast.11) | data formatting | bytes 7864320

commit v3 on v2

--- a/solution.py
+++ b/solution.py
@@ -73,10 +73,9 @@
         for side in range(2):
             second(k, side).start()
 
-        @pl.when(k + 1 < chunks)
-        def _():
-            for side in range(2):
-                first(k + 1, side).start()
+    def send(k):
+        for side in range(2):
+            first(k, side).start()
 
     def weights(g, slot, start):
         def copies(gate, up):
@@ -129,8 +128,7 @@
             n = e % (local // 2) * slots
             onehot[r, e // (local // 2), n : n + slots, :] = jnp.where(hit, 1.0, 0.0).astype(BF16)
 
-    for side in range(2):
-        first(0, side).start()
+    send(0)
     for k in range(members - 1):
         tokens_in(k, 0, k).start()
     for g in range(depth - 1):
@@ -146,9 +144,13 @@
         def _():
             tokens_in(k + members - 1, 0, (k + members - 1) % members).start()
 
-        @pl.when(k == (2 * chunks) // 3)
+        @pl.when(k == chunks - 3)
         def _():
             relay(0)
+
+        @pl.when(k == chunks - 1)
+        def _():
+            send(1)
 
         @pl.when(k == chunks - members)
         def _():
@@ -206,9 +208,13 @@
             g = head + k * steps + i
             slot = g % depth
 
-            @pl.when((i == steps // 5) & (k + 1 < chunks))
+            @pl.when((i == 3 * steps // 10) & (k + 1 < chunks))
             def _():
                 relay(k + 1)
+
+            @pl.when((i == 6 * steps // 10) & (k + 2 < chunks))
+            def _():
+                send(k + 2)
 
             @pl.when((i == (4 * steps) // 5) & (k + 1 < chunks))
             def _():
@@ -325,9 +331,22 @@
 
                 weights(g, slot, False)
                 weights(g + depth - 1, (g + depth - 1) % depth, True)
-                for i in range(group):
-                    v = dot(hbuf[group * p + i], wbuf[slot, i]).astype(BF16)
-                    outs[:, group * p + i] = v.reshape(members, slots, width)
+
+                def project():
+                    for i in range(group):
+                        v = dot(hbuf[group * p + i], wbuf[slot, i]).astype(BF16)
+                        outs[:, group * p + i] = v.reshape(members, slots, width)
+
+                early = (n == 0) & (p < 2)
+
+                @pl.when(early)
+                def _():
+                    mark(1 - p)
+                    project()
+
+                @pl.when(jnp.logical_not(early))
+                def _():
+                    project()
 
             def term(r):
                 return dot(comb[r], outs[r].reshape(local * slots, width))
@@ -340,11 +359,6 @@
             abuf[n % 2] = term(3).astype(BF16)
             for side in range(2):
                 across(n, side).start()
-
-            @pl.when(n == 0)
-            def _():
-                mark(1)
-                mark(0)
 
             g = n * steps + groups
             slot = g % depth

time: 362 us -> 360 us (level)
  no operation moved by 1% of the time
where the time goes in v3:
time: 360 us
  Pallas kernels  356 us (99%)
  local copies, waits for them, and re-layouts  4.29 us (1%)
    pallas_call x1, Pallas kernels, gather(): pl.pallas_call(lambda *refs: gather_kernel(members, *refs), name='gather_...  210 us
    pallas_call x1, Pallas kernels, scatter(): pl.pallas_call(lambda *refs: scatter_kernel(members, *refs), name='projec...  146 us

profile of v3, /device:TPU:112, one launch (start us, length us, event | category | flops | bytes accessed | tf_op | source)
XLA Modules:
  0.0 360.0 jit_solution(1087878212217941917)
XLA Ops:
  0.0 209.7 %gather_project.1 = (bf16[10,384,1536]{2,1,0:T(8,128)(2,1)}, bf16[384,1536]{1,0:T(8,128)(2,1)}, bf16[3,384,5120]{2,1,0:T(8,128)(2,1)}, f32[4,16,384]{2,1,0:T(8,128)}) custom-call(bf16[384,5120]{1,0:T(8,128)(2,1)} %bitcast.12, s32[8,384]{1,0:T(8,128)} %bitcast.13, s32[8,384]{1,0:T(8,128)} %bitcast.14, f32[8,384]{1,0:T(8,128)} %bitcast.15, ...), custom_call_target="tpu_custom_call" | custom-call | tf_op jit(solution)/shard_map/gather_project/pallas_call | solution.py:415
  209.7 146.0 %project_scatter.1 = bf16[384,5120]{1,0:T(8,128)(2,1)} custom-call(bf16[10,384,1536]{2,1,0:T(8,128)(2,1)} %get-tuple-element.8.refs_0_, bf16[384,1536]{1,0:T(8,128)(2,1)} %get-tuple-element.9.refs_1_, f32[4,16,384]{2,1,0:T(8,128)} %get-tuple-element.10.refs_2_, bf16[10,1536,5120]{2,1,0:T(8,128)(2,1)} %refs_3_.1, bf16[1536,5120]{1,0:T(8,128)(2,1)} %refs_4_.3), custom_call_target="tpu_custom_call" | custom-call | tf_op jit(solution)/shard_map/project_scatter/pallas_call | solution.py:448
  355.7 4.3 %copy.12 = bf16[1,1,384,5120]{3,2,1,0:T(8,128)(2,1)} copy(bf16[1,1,384,5120]{3,2,1,0:T(8,128)(2,1)} %bitcast.11) | data formatting | bytes 7864320
